TPU v7x, 32 devices: a whole 2x2x4 slice. The times are simulated.
32 devices in a mesh: ctx: 2 (over y), tp: 2 (over core), dec: 8 (over z, x).
Axes of the slice: x: 2, y: 2, z: 4, core: 2. Of those that a mesh axis runs over, the one named last changes fastest.
Arguments:
- cache: bfloat16 [8, 512, 576], P('dec', 'ctx'), may hold values from -6 to 6
- lengths: int32 [8], P('dec'), may hold values from 1 to 512
- slot_sequence: int32 [8], replicated, may hold values from 0 to 7, each once
- parents: int32 [8, 64], P('dec'), may hold values from 0 to 62, as said below
- query_nope: bfloat16 [8, 64, 128, 128], P('dec', None, 'tp'), may hold values from -6 to 6
- query_rope: bfloat16 [8, 64, 128, 64], P('dec', None, 'tp'), may hold values from -90 to 90
- new_latent: bfloat16 [8, 64, 576], P('dec'), may hold values from -6 to 6
- key_up: bfloat16 [128, 128, 512], P('tp'), may hold values from -0.5 to 0.5
- value_up: bfloat16 [128, 512, 128], P('tp'), may hold values from -0.25 to 0.25
- out_proj: bfloat16 [16384, 7168], P('tp', ('ctx', 'dec')), may hold values from -0.046875 to 0.046875
Outputs:
- attended: bfloat16 [8, 64, 7168], P(None, 'tp', ('ctx', 'dec'))
Inputs may be any that keep to these rules, and one draw needn't show every extreme that they name: `slot_sequence`: every sequence is held by exactly one slot. parents[s, 0] = 0 and parents[s, i] < i for every i >= 1.
All inputs are finite; a program needn't handle non-finite values.
Results may differ from a plain program's by a relative error of at most 0.024.
Values may be sent and summed in bfloat16 or wider, within the bound.
No kernel may reach another device: no remote copies, remote signals or barrier semaphores. Data moves between devices by JAX's collectives and lax.ppermute only.
A program may use at most 128 MiB of HBM per device.

v0:
```python
import math

import jax
import jax.numpy as jnp
from jax import lax
from jax.sharding import PartitionSpec as P


def combined_all(value, axis, combine):
    everything = jax.tree.map(
        lambda part, kind: lax.all_gather(part.astype(kind), axis),
        value,
        jax.tree.map(lambda a: jnp.bfloat16 if a.dtype == jnp.float32 else a.dtype, value),
    )

    def take(k):
        return jax.tree.map(lambda part, own: part[k].astype(own.dtype), everything, value)

    return lax.fori_loop(
        1, lax.axis_size(axis), lambda k, so_far: combine(so_far, take(k)), take(0)
    )


def ancestors(parents):
    node_count = parents.shape[-1]
    node_ids = jnp.arange(node_count, dtype=jnp.int32)
    parent_link = (parents[..., :, None] == node_ids).astype(jnp.float32)
    closure = jnp.maximum(parent_link, jnp.eye(node_count, dtype=jnp.float32))
    for _ in range(node_count.bit_length()):
        closure = jnp.minimum(
            jnp.einsum("sij,sjk->sik", closure, closure, precision=lax.Precision.HIGHEST), 1.0
        )
    return closure


def partial_softmax(queries, key_rows, live_mask, latent, score_scale):
    scores = (
        jnp.einsum("snhc,spc->snhp", queries, key_rows, preferred_element_type=jnp.float32)
        * score_scale
    )
    alive = live_mask > 0
    scores = jnp.where(alive, scores, -1e30)
    row_peak = jnp.max(scores, axis=-1)
    expo = jnp.where(alive, jnp.exp(scores - row_peak[..., None]), 0.0)
    row_total = jnp.sum(expo, axis=-1)
    weighted = jnp.einsum(
        "snhp,spc->snhc",
        expo.astype(jnp.bfloat16),
        key_rows[..., :latent],
        preferred_element_type=jnp.float32,
    )
    return (row_peak, row_total, weighted)


def join_parts(first_part, second_part):
    new_peak = jnp.maximum(first_part[0], second_part[0])
    first_factor = jnp.exp(first_part[0] - new_peak)
    second_factor = jnp.exp(second_part[0] - new_peak)
    row_total = first_part[1] * first_factor + second_part[1] * second_factor
    weighted = first_part[2] * first_factor[..., None] + second_part[2] * second_factor[..., None]
    return (new_peak, row_total, weighted)


def pick_rows(select, pieces):
    flat_rows = pieces.reshape(pieces.shape[0], -1)
    chosen = jnp.dot(select, flat_rows, preferred_element_type=jnp.float32)
    return chosen.reshape((select.shape[0],) + pieces.shape[1:]).astype(pieces.dtype)


def to_values(part, value_weight):
    projected = jnp.einsum("snhc,hcv->snhv", part[2], value_weight, precision=lax.Precision.HIGHEST)
    return (part[0], part[1], projected)


def on_device(
    cache,
    lengths,
    slot_sequence,
    parents,
    query_nope,
    query_rope,
    new_latent,
    key_up,
    value_up,
    out_proj,
):
    seq_dev = cache.shape[0]
    ctx_len = cache.shape[1]
    latent = value_up.shape[1]
    node_count = parents.shape[1]
    ctx_count = lax.axis_size("ctx")
    dec_count = lax.axis_size("dec")
    ctx_at = lax.axis_index("ctx")
    dec_at = lax.axis_index("dec")
    score_scale = 1.0 / math.sqrt(key_up.shape[1] + cache.shape[2] - latent)
    positions = ctx_at * ctx_len + jnp.arange(ctx_len, dtype=jnp.int32)
    valid = (positions[None, :] < lengths[:, None]).astype(jnp.bfloat16)
    tree_local = ancestors(parents).astype(jnp.bfloat16)
    value_weight = value_up.astype(jnp.float32)
    wanted = lax.dynamic_slice_in_dim(slot_sequence, dec_at * seq_dev, seq_dev)
    pieces = (
        lax.all_gather(cache, "dec", axis=0, tiled=True),
        lax.all_gather(valid, "dec", axis=0, tiled=True),
    )
    piece_count = pieces[0].shape[0]
    sources = jnp.arange(piece_count, dtype=jnp.int32)
    select = (wanted[:, None] == sources[None, :]).astype(jnp.bfloat16)
    key_rows = pick_rows(select, pieces[0])
    live_rows = pick_rows(select, pieces[1])
    nope_rows, rope_rows, tree_keys, tree_mask = (query_nope, query_rope, new_latent, tree_local)
    absorbed = jnp.einsum(
        "snhd,hdc->snhc", nope_rows, key_up, preferred_element_type=jnp.float32
    ).astype(jnp.bfloat16)
    queries = jnp.concatenate([absorbed, rope_rows], axis=-1)
    cache_part = partial_softmax(
        queries, key_rows, live_rows[:, None, None, :], latent, score_scale
    )
    cache_part = to_values(cache_part, value_weight)
    node_block = node_count // ctx_count
    first_node = ctx_at * node_block
    merged = combined_all(cache_part, "ctx", join_parts)
    merged = tuple(
        (lax.dynamic_slice_in_dim(member, first_node, node_block, 1) for member in merged)
    )
    block_queries = lax.dynamic_slice_in_dim(queries, first_node, node_block, 1)
    block_tree = lax.dynamic_slice_in_dim(tree_mask, first_node, node_block, 1)
    tree_part = partial_softmax(
        block_queries, tree_keys, block_tree[:, :, None, :], latent, score_scale
    )
    tree_part = to_values(tree_part, value_weight)
    final = join_parts(merged, tree_part)
    head_values = (final[2] / final[1][..., None]).astype(jnp.bfloat16)
    head_values = head_values.reshape(seq_dev, node_block, -1)
    projected = jnp.einsum(
        "ksnv,vd->ksnd",
        lax.all_gather(head_values[None], ("ctx", "dec"), axis=0, tiled=True),
        out_proj,
        preferred_element_type=jnp.float32,
    )
    column_count = out_proj.shape[1]
    projected = projected.reshape(ctx_count, dec_count, seq_dev, node_block, column_count)
    projected = projected.transpose(1, 2, 0, 3, 4).reshape(
        dec_count * seq_dev, node_count, column_count
    )
    return lax.psum_scatter(projected.astype(jnp.bfloat16), "tp", scatter_dimension=1, tiled=True)


def solution(mesh):
    return jax.shard_map(
        on_device,
        mesh=mesh,
        in_specs=(
            P("dec", "ctx", None),
            P("dec"),
            P(),
            P("dec", None),
            P("dec", None, "tp", None),
            P("dec", None, "tp", None),
            P("dec", None, None),
            P("tp", None, None),
            P("tp", None, None),
            P("tp", ("ctx", "dec")),
        ),
        out_specs=P(None, "tp", ("ctx", "dec")),
        check_vma=False,
    )
```

profile of v0, /device:TPU:0, one launch (start us, length us, event | category | flops | bytes accessed | tf_op | source)
XLA Modules:
  0.0 281.7 jit_solution(1390820935935153602)
XLA Ops:
  6.5 0.7 all-gather.8.cloned.1.call-update
  7.3 1.9 copy.32
  9.9 1.3 dynamic_slice.28
  11.1 22.4 %all-gather.3 = bf16[8,1,256]{2,1,0:T(2,128)(2,1)S(1)} all-gather(bf16[1,1,256]{2,1,0:T(2,128)(2,1)S(1)} %fusion.70), channel_id=1, replica_groups=mesh['ctx'=2,'tp'=2,'dec'=8] {'dec'}, dimensions={0}, use_global_device_ids=true | all-gather | bytes 4608 | tf_op jit(solution)/shard_map/all_gather | solution.py:103
  33.5 0.6 bitcast_convert_fusion
  34.2 0.8 fusion.49
  35.0 0.2 convolution_minimum_fusion.5
  35.2 0.2 convolution_minimum_fusion.4
  35.3 0.2 convolution_minimum_fusion.3
  35.5 0.2 convolution_minimum_fusion.2
  35.7 0.2 convolution_minimum_fusion.1
  35.8 0.2 convolution_minimum_fusion
  36.0 0.2 fusion.75
  36.2 5.5 %convert_bitcast_fusion = bf16[1,64,64,512]{3,1,2,0:T(8,128)(2,1)S(1)} fusion(bf16[64,128,512]{2,1,0:T(8,128)(2,1)} %param.17, bf16[64,64,128]{2,1,0:T(8,128)(2,1)} %bitcast.165), kind=kOutput, calls=%fused_computation.12 | convolution fusion | flops 538968064 | bytes 13631488 | tf_op jit(solution)/shard_map/snhd,hdc->snhc/dot_general | solution.py:111
  41.7 1.8 fusion.9
  43.5 0.8 fusion.65
  44.2 3.1 %fusion.3 = bf16[64,64,576]{2,0,1:T(8,128)(2,1)} fusion(bf16[1,64,64,64]{3,1,2,0:T(8,128)(2,1)S(1)} %copy.32, bf16[1,64,64,512]{3,1,2,0:T(8,128)(2,1)S(1)} %convert_bitcast_fusion), kind=kLoop, calls=%fused_computation.5 | loop fusion | flops 9437184 | bytes 9437184 | tf_op jit(solution)/shard_map/reshape.15
  47.3 16.8 %all-gather.8.cloned.1.call-done = bf16[8,256,576]{1,2,0:T(8,128)(2,1)} async-done(((bf16[1,256,576]{1,2,0:T(8,128)(2,1)}), bf16[8,256,576]{1,2,0:T(8,128)(2,1)}) %all-gather.8.cloned.1.call-update) | async-done | bytes 2359312 | tf_op jit(solution)/shard_map/all_gather | solution.py:102
  64.1 3.1 %copy.33 = bf16[8,256,576]{2,1,0:T(8,128)(2,1)S(1)} copy(bf16[8,256,576]{1,2,0:T(8,128)(2,1)} %all-gather.8.cloned.1.call-done) | data formatting | bytes 4718592 | tf_op jit(solution)/shard_map/all_gather | solution.py:102
  67.2 4.1 %reshape.549 = bf16[1179648]{0:T(1024)(128)(2,1)} reshape(bf16[8,256,576]{2,1,0:T(8,128)(2,1)S(1)} %copy.33) | data formatting | bytes 4718592
  71.3 2.7 reshape.501
  74.0 2.5 reshape.551
  76.6 4.5 %reshape.552 = bf16[8,256,576]{2,1,0:T(8,128)(2,1)S(1)} reshape(bf16[1179648]{0:T(1024)(128)(2,1)} %reshape.551) | data formatting | bytes 4718592
  81.1 0.6 multiply_reduce_fusion
  81.7 9.1 %fusion.6 = (f32[64,64]{1,0:T(8,128)S(1)}, f32[64,64,256]{2,1,0:T(8,128)S(1)}) fusion(pred[256]{0:T(512)(128)(4,1)S(1)} %convert_compare_fusion, bf16[256,576]{1,0:T(8,128)(2,1)S(1)} %multiply_reduce_fusion, bf16[64,64,576]{2,0,1:T(8,128)(2,1)} %fusion.3), kind=kOutput, calls=%fused_computation.13 | convolution fusion | flops 1211101184 | bytes 9224448 | tf_op jit(solution)/shard_map/snhc,spc->snhp/dot_general | solution.py:38
  90.8 1.9 fusion.7
  92.8 1.8 fusion.13
  94.5 0.5 slice-done.1
  95.0 4.7 %fusion.15 = bf16[1,64,64,128]{3,1,2,0:T(8,128)(2,1)S(1)} fusion(f32[64,64,512]{2,0,1:T(8,128)S(1)} %fusion.13, bf16[64,512,128]{2,1,0:T(8,128)(2,1)S(1)} %bitcast.162), kind=kOutput, calls=%fused_computation.23 | convolution fusion | flops 3221749760 | bytes 17825792 | tf_op jit(solution)/shard_map/snhc,hcv->snhv/dot_general | solution.py:71
  99.7 1.6 copy.37
  101.4 2.8 %fusion.74 = (f32[32,64]{1,0:T(8,128)S(1)}, f32[32,64,64]{1,2,0:T(8,128)S(1)}) fusion(bf16[1,64,576]{2,1,0:T(8,128)(2,1)S(1)} %copy-done.2, bf16[1,32,64,576]{3,1,2,0:T(8,128)(2,1)S(1)} %copy-done.1, pred[32,64]{1,0:T(8,128)(4,1)S(1)} %fusion.61), kind=kOutput, calls=%fused_computation.104 | convolution fusion | flops 151386112 | bytes 2967552 | tf_op jit(solution)/shard_map/snhc,spc->snhp/dot_general | solution.py:38
  104.3 0.5 fusion.39
  104.7 0.8 copy.44
  105.5 2.6 fusion.44
  108.1 4.9 %all-gather.2 = bf16[128,64]{1,0:T(8,128)(2,1)S(1)} all-gather(bf16[64,64]{1,0:T(8,128)(2,1)S(1)} %get-tuple-element.19), channel_id=4, replica_groups=mesh['ctx'=2,'tp'=2,'dec'=8] {'ctx'}, dimensions={0}, use_global_device_ids=true | all-gather | bytes 24576 | tf_op jit(solution)/shard_map/all_gather | solution.py:11
  113.0 4.9 %all-gather.1 = bf16[128,64]{1,0:T(8,128)(2,1)S(1)} all-gather(bf16[64,64]{1,0:T(8,128)(2,1)S(1)} %convert_element_type.285), channel_id=3, replica_groups=mesh['ctx'=2,'tp'=2,'dec'=8] {'ctx'}, dimensions={0}, use_global_device_ids=true | all-gather | bytes 24576 | tf_op jit(solution)/shard_map/all_gather | solution.py:11
  117.9 0.1 copy.43
  118.4 0.1 constant_dynamic-slice_fusion
  118.5 15.2 %all-gather.12.cloned.1.call-done = bf16[2,64,64,128]{3,2,1,0:T(8,128)(2,1)} async-done(((bf16[1,64,64,128]{3,2,1,0:T(8,128)(2,1)}), bf16[2,64,64,128]{3,2,1,0:T(8,128)(2,1)}) %all-gather.12.cloned.1.call-update) | async-done | bytes 2097168 | tf_op jit(solution)/shard_map/all_gather | solution.py:11
  133.7 1.9 fusion.73
  135.6 0.9 copy-done
  136.5 7.8 %fusion.25 = bf16[1,32,64,128]{3,1,2,0:T(8,128)(2,1)S(1)} fusion(f32[32,64,512]{2,0,1:T(8,128)S(1)} %copy-done, bf16[64,512,128]{2,1,0:T(8,128)(2,1)} %param.18, bf16[1,32,64,128]{3,2,1,0:T(8,128)(2,1)S(1)} %get-tuple-element.50, bf16[1,32,64,128]{3,2,1,0:T(8,128)(2,1)S(1)} %get-tuple-element.51, f32[32,64]{0,1:T(8,128)S(1)} %get-tuple-element.49, ...), kind=kOutput, calls=%fused_computation.30 | convolution fusion | flops 1613234176 | bytes 14196736 | tf_op jit(solution)/shard_map/snhc,hcv->snhv/dot_general | solution.py:71
  144.3 0.2 copy.47
  144.5 1.0 broadcast_in_dim_reshape.3
  145.6 112.4 %all-gather.10.cloned.1.call-done = bf16[16,1,32,8192]{3,2,1,0:T(8,128)(2,1)} async-done(((bf16[1,1,32,8192]{3,2,1,0:T(8,128)(2,1)}), bf16[16,1,32,8192]{3,2,1,0:T(8,128)(2,1)}) %all-gather.10.cloned.1.call-update) | async-done | bytes 8388624 | tf_op jit(solution)/shard_map/all_gather | solution.py:136
  258.0 10.0 %fusion.31 = bf16[8,1,2,32,448]{4,3,0,2,1:T(8,128)(2,1)S(1)} fusion(bf16[8192,448]{0,1:T(8,128)(2,1)} %param.19, bf16[2,8,32,8192]{3,2,1,0:T(8,128)(2,1)} %bitcast.169), kind=kOutput, calls=%fused_computation.32 | convolution fusion | flops 3758325760 | bytes 16187392 | tf_op jit(solution)/shard_map/ksnv,vd->ksnd/dot_general | solution.py:134
  268.0 0.8 copy.48
  268.9 6.3 %reduce-scatter.2.cloned.1.call-done = bf16[8,32,448]{2,1,0:T(8,128)(2,1)} async-done(((bf16[8,64,448]{2,1,0:T(8,128)(2,1)}), bf16[8,32,448]{2,1,0:T(8,128)(2,1)}) %reduce-scatter.2.cloned.1.call-update) | async-done | bytes 229392 | tf_op jit(solution)/shard_map/reduce_scatter | solution.py:145
  (30 shorter events, 0.7 us)
Async XLA Ops:
  6.5 57.6 %all-gather.8.cloned.1.call-start = ((), (), s32[]{:S(2)}) async-start(), calls=%async_computation.1 | async-start | bytes 2654208 | tf_op jit(solution)/shard_map/all_gather | solution.py:102
  7.3 126.4 %all-gather.12.cloned.1.call-start = ((), (), s32[]{:S(2)}) async-start(), calls=%async_computation.4 | async-start | bytes 3145728 | tf_op jit(solution)/shard_map/all_gather | solution.py:11
  90.8 3.7 %slice-start = ((s8[8388608]{0:T(1024)(128)(4,1)}), s8[4194304]{0:T(1024)(128)(4,1)S(1)}, s32[]{:S(2)}) async-start(s8[8388608]{0:T(1024)(128)(4,1)} %bitcast.161), calls=%async_computation.5 | async-start | bytes 8388608
  92.7 2.3 slice-start.1
  95.0 6.4 %copy-start.1 = (bf16[1,32,64,576]{3,1,2,0:T(8,128)(2,1)S(1)}, bf16[1,32,64,576]{3,1,2,0:T(8,128)(2,1)}, u32[]{:S(2)}) copy-start(bf16[1,32,64,576]{3,1,2,0:T(8,128)(2,1)} %fusion.9) | copy-start | bytes 7077892
  95.0 6.4 %copy-start.2 = (bf16[1,64,576]{2,1,0:T(8,128)(2,1)S(1)}, bf16[1,64,576]{2,1,0:T(8,128)(2,1)}, u32[]{:S(2)}) copy-start(bf16[1,64,576]{2,1,0:T(8,128)(2,1)} %param.16) | copy-start | bytes 221188
  101.3 156.7 %all-gather.10.cloned.1.call-start = ((), (), s32[]{:S(2)}) async-start(), calls=%async_computation.2 | async-start | bytes 8912896 | tf_op jit(solution)/shard_map/all_gather | solution.py:136
  133.7 2.8 %copy-start = (f32[32,64,512]{2,0,1:T(8,128)S(1)}, f32[32,64,512]{2,0,1:T(8,128)}, u32[]{:S(2)}) copy-start(f32[32,64,512]{2,0,1:T(8,128)} %fusion.44) | copy-start | bytes 12582916
  145.6 129.6 %reduce-scatter.2.cloned.1.call-start = ((), (), s32[]{:S(2)}) async-start(), calls=%async_computation.3 | async-start | bytes 786432 | tf_op jit(solution)/shard_map/reduce_scatter | solution.py:145
Sparse Core Ops, SparseCore 0:
  9.5 54.5 all-gather.7
  101.5 32.1 all-gather.11
  145.7 112.2 all-gather.9
  269.0 6.0 reduce-scatter.1
where the time goes:
time: 282 us
  waiting for transfers between devices  151 us (54%)
  matrix products  46.2 us (16%)
  blocking collectives  32.1 us (11%)
  local copies, waits for them, and re-layouts  28.4 us (10%)
  between operations  14 us (5%)
  other arithmetic  9.44 us (3%)
    all_gather x1, waiting for transfers between devices, on_device(): lax.all_gather(head_values[None], ('ctx', 'dec'), axis=0, tiled=True)  112 us
    all_gather x1, blocking collectives, on_device(): lax.all_gather(valid, 'dec', axis=0, tiled=True)  22.4 us
    all_gather x1, waiting for transfers between devices, on_device(): lax.all_gather(cache, 'dec', axis=0, tiled=True)  16.8 us
    all_gather x1, waiting for transfers between devices, combined_all(): lax.all_gather(part.astype(kind), axis)  15.2 us
    unnamed x15, local copies, waits for them, and re-layouts  14.5 us
    dot_general x2, matrix products, to_values(): jnp.einsum('snhc,hcv->snhv', part[2], value_weight, precision=lax.Precisi...  12.5 us
    dot_general x2, matrix products, partial_softmax(): jnp.einsum('snhc,spc->snhp', queries, key_rows, preferred_element_type=jn...  12 us
    dot_general x1, matrix products, on_device(): jnp.einsum('ksnv,vd->ksnd', lax.all_gather(head_values[None], ('ctx', 'de...  9.97 us
  transfers between devices with their start and end apart: 4, of which 4 were waited for; matrix products, arithmetic and copies ran while one was open for 9% of the time, Pallas kernels for 0%

commit v1 on v0

v1 whole, which is shorter than its diff:
```python
import math

import jax
import jax.numpy as jnp
from jax import lax
from jax.experimental import pallas as pl
from jax.experimental.pallas import tpu as pltpu
from jax.sharding import PartitionSpec as P

NEG = -1e30
F32 = jnp.float32
BF16 = jnp.bfloat16
NT = (((1,), (1,)), ((), ()))


def bit_list(count):
    return [1 << k for k in range(count.bit_length() - 1)]


def swap(value, axis, mask):
    count = lax.axis_size(axis)
    return lax.ppermute(value, axis, [(i, i ^ mask) for i in range(count)])


def round_up(value, unit):
    return -(-value // unit) * unit


def tree_kernel(spots_ref, parents_ref, latent_ref, out_ref):
    nodes, feat = latent_ref.shape
    extra = out_ref.shape[1] - feat
    first = spots_ref[0]
    block = spots_ref[1]
    row = lax.broadcasted_iota(jnp.int32, (nodes, nodes), 0)
    col = lax.broadcasted_iota(jnp.int32, (nodes, nodes), 1)
    linked = (parents_ref[...] == row) | (row == col)
    closure = jnp.where(linked, 1.0, 0.0)
    for _ in range((nodes - 1).bit_length()):
        packed = closure.astype(BF16)
        closure = jnp.minimum(jnp.dot(packed, packed, preferred_element_type=F32), 1.0)
    row = lax.broadcasted_iota(jnp.int32, (nodes, extra), 0)
    col = lax.broadcasted_iota(jnp.int32, (nodes, extra), 1)
    pick = jnp.where(row == first + col - 1, 1.0, 0.0).astype(BF16)
    seen = jnp.dot(closure.astype(BF16), pick, preferred_element_type=F32)
    barred = (col >= 1) & (col <= block) & (seen < 0.5)
    out_ref[:, :feat] = latent_ref[...]
    out_ref[:, feat:] = jnp.where(barred, NEG, 0.0).astype(BF16)


def absorb_kernel(nope_ref, rope_ref, key_up_ref, out_ref):
    heads, nodes, _ = nope_ref.shape
    latent = key_up_ref.shape[2]
    feat = latent + rope_ref.shape[2]
    extra = out_ref.shape[2] - feat
    row = lax.broadcasted_iota(jnp.int32, (nodes, extra), 0)
    col = lax.broadcasted_iota(jnp.int32, (nodes, extra), 1)
    marks = jnp.where((col == 0) | (col == row + 1), 1.0, 0.0).astype(BF16)
    for h in range(heads):
        absorbed = jnp.dot(nope_ref[h], key_up_ref[h], preferred_element_type=F32)
        out_ref[h, :, :latent] = absorbed.astype(BF16)
        out_ref[h, :, latent:feat] = rope_ref[h]
        out_ref[h, :, feat:] = marks


def attend_kernel(score_scale, *refs):
    query_ref, tree_ref, value_ref = refs[:3]
    key_refs = refs[3:-1]
    out_ref = refs[-1]
    heads, nodes, width = query_ref.shape
    latent = value_ref.shape[1]
    depth = value_ref.shape[2]
    queries = query_ref[...].reshape(heads * nodes, width)
    scores = [jnp.dot(queries, key_ref[...], preferred_element_type=F32) for key_ref in key_refs]
    scores.append(lax.dot_general(queries, tree_ref[...], NT, preferred_element_type=F32))
    peak = scores[0].max(axis=-1, keepdims=True)
    for part in scores[1:]:
        peak = jnp.maximum(peak, part.max(axis=-1, keepdims=True))
    factor = score_scale * math.log2(math.e)
    expos = [jnp.exp2((part - peak) * factor) for part in scores]
    total = expos[0].sum(axis=-1, keepdims=True)
    for part in expos[1:]:
        total = total + part.sum(axis=-1, keepdims=True)
    weighted = jnp.dot(expos[-1].astype(BF16), tree_ref[:, :latent], preferred_element_type=F32)
    for part, key_ref in zip(expos, key_refs):
        weighted = weighted + lax.dot_general(
            part.astype(BF16), key_ref[:latent, :], NT, preferred_element_type=F32
        )
    weighted = weighted.astype(BF16)
    share = 1.0 / total
    for h in range(heads):
        rows = slice(h * nodes, (h + 1) * nodes)
        projected = jnp.dot(weighted[rows], value_ref[h], preferred_element_type=F32)
        out_ref[:, h * depth : (h + 1) * depth] = (projected * share[rows]).astype(BF16)


def project_kernel(*refs):
    part_refs, weight_ref, out_ref = refs[:-2], refs[-2], refs[-1]
    rows = jnp.concatenate([ref[...] for ref in part_refs], axis=0)
    product = lax.dot_general(rows, weight_ref[...], NT, preferred_element_type=F32)

    @pl.when(pl.program_id(0) == 0)
    def _():
        out_ref[...] = product

    @pl.when(pl.program_id(0) > 0)
    def _():
        out_ref[...] += product


def collect_kernel(places, block, spots_ref, *refs):
    out_ref = refs[-1]
    for (dec_mask, ctx_mask), entries in places.items():
        total = None
        for index, offset in entries:
            part = refs[index][offset : offset + block, :]
            total = part if total is None else total + part
        slot = spots_ref[0] ^ dec_mask
        first = pl.multiple_of((spots_ref[1] ^ ctx_mask) * block, block)
        out_ref[slot, pl.ds(first, block), :] = total


def whole_spec(shape):
    return pl.BlockSpec(shape, lambda *_: (0,) * len(shape))


SMEM_SPEC = pl.BlockSpec(memory_space=pltpu.SMEM)


def on_device(
    cache,
    lengths,
    slot_sequence,
    parents,
    query_nope,
    query_rope,
    new_latent,
    key_up,
    value_up,
    out_proj,
):
    ctx_count = lax.axis_size("ctx")
    dec_count = lax.axis_size("dec")
    tp_count = lax.axis_size("tp")
    ctx_at = lax.axis_index("ctx")
    dec_at = lax.axis_index("dec")
    tp_at = lax.axis_index("tp")
    rows = cache.shape[1]
    feat = cache.shape[2]
    heads, head_size, latent = key_up.shape
    depth = value_up.shape[2]
    nodes = parents.shape[1]
    node_block = nodes // ctx_count
    first_node = ctx_at * node_block
    columns = out_proj.shape[1]
    width = round_up(feat + 1 + node_block, 128)
    score_scale = 1.0 / math.sqrt(head_size + feat - latent)
    row_block = rows // tp_count

    positions = ctx_at * rows + jnp.arange(rows, dtype=jnp.int32)
    bias = jnp.where(positions < lengths[0], 0.0, NEG).astype(BF16)[None, :]
    keys = jnp.concatenate([cache[0].T, bias, jnp.zeros((width - feat - 1, rows), BF16)], axis=0)
    keys = lax.dynamic_slice_in_dim(keys, tp_at * row_block, row_block, 1)
    pieces = keys.reshape(dec_count, width // dec_count, row_block)
    pieces = lax.all_to_all(pieces, "dec", 0, 0, tiled=True)
    pieces = jnp.stack(
        [lax.dynamic_index_in_dim(pieces, slot_sequence[k], 0, False) for k in range(dec_count)]
    )
    pieces = lax.all_to_all(pieces, "dec", 0, 0, tiled=True)
    keys = pieces.reshape(width, row_block)
    for mask in bit_list(ctx_count):
        keys = jnp.concatenate([keys, swap(keys, "ctx", mask)], axis=1)
    key_parts = [keys]
    for mask in bit_list(tp_count):
        sent = keys if len(key_parts) == 1 else jnp.concatenate(key_parts, axis=1)
        key_parts = [sent, swap(sent, "tp", mask)]

    spots = jnp.stack([first_node, jnp.int32(node_block)])
    tree = pl.pallas_call(
        tree_kernel,
        in_specs=[SMEM_SPEC, whole_spec((1, nodes)), whole_spec((nodes, feat))],
        out_specs=whole_spec((nodes, width)),
        out_shape=jax.ShapeDtypeStruct((nodes, width), BF16),
        grid=(1,),
        name="tree_keys",
    )(spots, parents, new_latent[0])

    head_step = min(8, heads)
    nope = lax.dynamic_slice_in_dim(query_nope[0], first_node, node_block, 0).transpose(1, 0, 2)
    rope = lax.dynamic_slice_in_dim(query_rope[0], first_node, node_block, 0).transpose(1, 0, 2)
    queries = pl.pallas_call(
        absorb_kernel,
        grid=(heads // head_step,),
        in_specs=[
            pl.BlockSpec((head_step, node_block, head_size), lambda i: (i, 0, 0)),
            pl.BlockSpec((head_step, node_block, feat - latent), lambda i: (i, 0, 0)),
            pl.BlockSpec((head_step, head_size, latent), lambda i: (i, 0, 0)),
        ],
        out_specs=pl.BlockSpec((head_step, node_block, width), lambda i: (i, 0, 0)),
        out_shape=jax.ShapeDtypeStruct((heads, node_block, width), BF16),
        cost_estimate=pl.CostEstimate(
            flops=4 * heads * node_block * head_size * latent,
            bytes_accessed=2 * heads * head_size * latent,
            transcendentals=0,
        ),
        name="absorb",
    )(nope, rope, key_up)

    class_heads = heads // 2
    step = min(head_step, class_heads)
    key_rows = sum(part.shape[1] for part in key_parts)

    def attend(which):
        base = which * (class_heads // step)
        return pl.pallas_call(
            lambda *refs: attend_kernel(score_scale, *refs),
            grid=(class_heads // step,),
            in_specs=[
                pl.BlockSpec((step, node_block, width), lambda i: (base + i, 0, 0)),
                whole_spec((nodes, width)),
                pl.BlockSpec((step, latent, depth), lambda i: (base + i, 0, 0)),
            ]
            + [whole_spec(part.shape) for part in key_parts],
            out_specs=pl.BlockSpec((node_block, step * depth), lambda i: (0, i)),
            out_shape=jax.ShapeDtypeStruct((node_block, class_heads * depth), BF16),
            cost_estimate=pl.CostEstimate(
                flops=2 * class_heads * node_block * (key_rows + nodes) * (width + latent),
                bytes_accessed=2 * class_heads * latent * depth,
                transcendentals=class_heads * node_block * key_rows,
            ),
            name="attend_%d" % which,
        )(queries, tree, value_up, *key_parts)

    dec_bits = [("dec", bit) for bit in bit_list(dec_count)]
    ctx_bits = [("ctx", bit) for bit in bit_list(ctx_count)]
    orders = (
        dec_bits[2:] + dec_bits[:1] + dec_bits[1:2] + ctx_bits,
        dec_bits[2:] + ctx_bits + dec_bits[1:2] + dec_bits[:1],
    )

    weight = out_proj.T
    class_depth = class_heads * depth
    depth_step = min(1024, class_depth)
    depth_steps = class_depth // depth_step

    def project(parts, which):
        count = len(parts)
        return pl.pallas_call(
            project_kernel,
            grid=(depth_steps,),
            in_specs=[pl.BlockSpec((node_block, depth_step), lambda i: (0, i))] * count
            + [pl.BlockSpec((columns, depth_step), lambda i: (0, which * depth_steps + i))],
            out_specs=whole_spec((count * node_block, columns)),
            out_shape=jax.ShapeDtypeStruct((count * node_block, columns), F32),
            cost_estimate=pl.CostEstimate(
                flops=2 * count * node_block * class_depth * columns,
                bytes_accessed=2 * class_depth * columns,
                transcendentals=0,
            ),
            name="project_%d" % which,
        )(*parts, weight)

    places = {}
    results = []
    waves = []
    held = [{(0, 0): attend(which)} for which in range(2)]
    for level in range(len(orders[0])):
        for which in range(2):
            axis, mask = orders[which][level]
            fresh = {}
            for (dec_mask, ctx_mask), part in held[which].items():
                spot = (dec_mask ^ mask, ctx_mask) if axis == "dec" else (dec_mask, ctx_mask ^ mask)
                fresh[spot] = swap(part, axis, mask)
            if level == len(orders[0]) - 1:
                waves.append((which, held[which]))
                waves.append((which, fresh))
            held[which] = {**held[which], **fresh}
    for which, parts in waves:
        index = len(results)
        results.append(project(list(parts.values()), which))
        for k, spot in enumerate(parts):
            places.setdefault(spot, []).append((index, k * node_block))

    here = jnp.stack([dec_at, ctx_at])
    partial = pl.pallas_call(
        lambda *refs: collect_kernel(places, node_block, *refs),
        in_specs=[SMEM_SPEC] + [whole_spec(part.shape) for part in results],
        out_specs=whole_spec((dec_count, nodes, columns)),
        out_shape=jax.ShapeDtypeStruct((dec_count, nodes, columns), F32),
        grid=(1,),
        name="collect",
    )(here, *results)
    if tp_count != 2:
        return lax.psum_scatter(partial.astype(BF16), "tp", scatter_dimension=1, tiled=True)
    half = nodes // 2
    away = lax.dynamic_slice_in_dim(partial, (1 - tp_at) * half, half, 1).astype(BF16)
    kept = lax.dynamic_slice_in_dim(partial, tp_at * half, half, 1)
    return (kept + swap(away, "tp", 1).astype(F32)).astype(BF16)


def solution(mesh):
    return jax.shard_map(
        on_device,
        mesh=mesh,
        in_specs=(
            P("dec", "ctx", None),
            P("dec"),
            P(),
            P("dec", None),
            P("dec", None, "tp", None),
            P("dec", None, "tp", None),
            P("dec", None, None),
            P("tp", None, None),
            P("tp", None, None),
            P("tp", ("ctx", "dec")),
        ),
        out_specs=P(None, "tp", ("ctx", "dec")),
        check_vma=False,
    )
```

time: 282 us -> 170 us (0.60)
  waiting for transfers between devices: 151 us -> 46.5 us
  Pallas kernels: 0 us -> 48.3 us
  matrix products: 46.2 us -> 0 us
  starting transfers between devices: 0.12 us -> 32.1 us
  local copies, waits for them, and re-layouts: 28.4 us -> 7.08 us
  blocking collectives: 32.1 us -> 13.4 us
  other arithmetic: 9.44 us -> 4.8 us
    all_gather x3 -> x0, waiting for transfers between devices: 144 us -> none  [the longest x1 112 us: on_device(): lax.all_gather(head_values[None], ('ctx', 'dec'), axis=0, tiled=True)]
    pallas_call x0 -> x9, Pallas kernels: none -> 48.3 us  [the longest x4 21.1 us: project(): pl.pallas_call(project_kernel, grid=(depth_steps,), in_specs=[pl.BlockSpe...]
    ppermute x0 -> x33, waiting for transfers between devices: none -> 46.5 us  [swap(): return lax.ppermute(value, axis, [(i, i ^ mask) for i in range(count)])]
    dot_general x16 -> x0, matrix products: 46.2 us -> none  [the longest x2 12.5 us: to_values(): jnp.einsum('snhc,hcv->snhv', part[2], value_weight, precision=lax.Precisi...]
    all_gather x3 -> x0, blocking collectives: 32.1 us -> none  [the longest x1 22.4 us: on_device(): lax.all_gather(valid, 'dec', axis=0, tiled=True)]
    ppermute x0 -> x33, starting transfers between devices: none -> 24.8 us  [swap(): return lax.ppermute(value, axis, [(i, i ^ mask) for i in range(count)])]
    unnamed x15 -> x43, local copies, waits for them, and re-layouts: 14.5 us -> 0.89 us
    all_to_all x0 -> x1, blocking collectives: none -> 13.4 us  [on_device(): pieces = lax.all_to_all(pieces, 'dec', 0, 0, tiled=True)]
  transfers between devices with their start and end apart: 4 -> 34, of which waited for: 4 -> 18; matrix products, arithmetic and copies ran while one was open for 9% -> 4% of each run, Pallas kernels for 0% -> 20%
where the time goes in v1:
time: 170 us; the launch traced here: 168 us
  Pallas kernels  48.3 us (28%)
  waiting for transfers between devices  46.5 us (27%)
  starting transfers between devices  32.1 us (19%)
  between operations  16 us (9%)
  blocking collectives  13.4 us (8%)
  local copies, waits for them, and re-layouts  7.08 us (4%)
  other arithmetic  4.8 us (3%)
    ppermute x33, waiting for transfers between devices, swap(): return lax.ppermute(value, axis, [(i, i ^ mask) for i in range(count)])  46.5 us
    ppermute x33, starting transfers between devices, swap(): return lax.ppermute(value, axis, [(i, i ^ mask) for i in range(count)])  24.8 us
    pallas_call x4, Pallas kernels, project(): pl.pallas_call(project_kernel, grid=(depth_steps,), in_specs=[pl.BlockSpe...  21.1 us
    pallas_call x2, Pallas kernels, attend(): pl.pallas_call(lambda *refs: attend_kernel(score_scale, *refs), grid=(cla...  13.9 us
    all_to_all x1, blocking collectives, on_device(): pieces = lax.all_to_all(pieces, 'dec', 0, 0, tiled=True)  13.4 us
    pallas_call x1, Pallas kernels, on_device(): pl.pallas_call(absorb_kernel, grid=(heads // head_step,), in_specs=[pl.Bl...  8.21 us
    all_to_all x1, starting transfers between devices, on_device(): pieces = lax.all_to_all(pieces, 'dec', 0, 0, tiled=True)  7.28 us
  transfers between devices with their start and end apart: 34, of which 18 were waited for; matrix products, arithmetic and copies ran while one was open for 4% of the time, Pallas kernels for 20%

profile of v1, /device:TPU:0, one launch (start us, length us, event | category | flops | bytes accessed | tf_op | source)
XLA Modules:
  0.0 168.2 jit_solution(14719472648730747198)
XLA Ops:
  0.8 1.7 %fusion.1 = bf16[640,128]{1,0:T(8,128)(2,1)} fusion(s32[]{:T(128)S(6)} %select_n.51, bf16[576,256]{1,0:T(8,128)(2,1)} %bitcast.38, bf16[1,256]{1,0:T(2,128)(2,1)S(1)} %fusion.2, bf16[640]{0:T(1024)(128)(2,1)S(1)} %pad.4.clone), kind=kLoop, calls=%fused_computation.8 | loop fusion | flops 491520 | bytes 460548 | tf_op jit(solution)/shard_map/concatenate | solution.py:161
  2.6 7.3 %all-to-all-start = ((bf16[8,80,128]{2,1,0:T(8,128)(2,1)}), bf16[8,80,128]{2,1,0:T(8,128)(2,1)S(1)}, u32[]{:S(2)}, u32[]{:S(2)}) async-start(bf16[8,80,128]{2,1,0:T(8,128)(2,1)} %bitcast.11), calls=%async_computation | async-start | bytes 327680 | tf_op jit(solution)/shard_map/all_to_all | solution.py:164
  9.9 1.6 fusion.3
  26.6 13.4 %all_to_all.10 = bf16[8,80,128]{2,1,0:T(8,128)(2,1)S(1)} all-to-all(bf16[8,80,128]{2,1,0:T(8,128)(2,1)S(1)} %dynamic-slice_dynamic-update-slice_fusion), channel_id=1, replica_groups=mesh['ctx'=2,'tp'=2,'dec'=8] {'dec'}, dimensions={0} | all-to-all | bytes 327680 | tf_op jit(solution)/shard_map/all_to_all | solution.py:168
  40.0 1.5 collective-permute-start
  41.5 3.8 %collective-permute-done = bf16[640,128]{1,0:T(8,128)(2,1)S(1)} collective-permute-done((bf16[640,128]{1,0:T(8,128)(2,1)S(1)}, bf16[640,128]{1,0:T(8,128)(2,1)S(1)}, u32[]{:S(2)}, u32[]{:S(2)}) %collective-permute-start) | collective-permute-done | bytes 163872 | tf_op jit(solution)/shard_map/ppermute | solution.py:22
  45.5 1.1 copy.16
  46.6 1.1 constant_dynamic-slice_fusion
  47.7 1.1 copy.15
  49.5 2.5 %tree_keys.1.refs_1_ = bf16[64,640]{1,0:T(8,128)(2,1)} custom-call(s32[2]{0:T(128)} %pad_add_fusion.1.spots_ref, s32[1,64]{1,0:T(1,128)} %parents_ref.1, bf16[64,576]{1,0:T(8,128)(2,1)} %bitcast.39), custom_call_target="tpu_custom_call" | custom-call | tf_op jit(solution)/shard_map/tree_keys/pallas_call | solution.py:178
  52.0 8.2 %absorb.1.refs_0_ = bf16[64,32,640]{2,1,0:T(8,128)(2,1)} custom-call(bf16[64,32,128]{2,1,0:T(8,128)(2,1)} %bitcast.34, bf16[64,32,64]{2,1,0:T(8,128)(2,1)} %bitcast.35, bf16[64,128,512]{2,1,0:T(8,128)(2,1)} %key_up_ref.1), custom_call_target="tpu_custom_call" | custom-call | flops 536870912 | bytes 8388608 | tf_op jit(solution)/shard_map/absorb/pallas_call | solution.py:190
  60.9 6.9 %attend_0.1.refs_0_ = bf16[32,4096]{1,0:T(8,128)(2,1)} custom-call(bf16[64,32,640]{2,1,0:T(8,128)(2,1)} %absorb.1.refs_0_, bf16[64,640]{1,0:T(8,128)(2,1)} %tree_keys.1.refs_1_, bf16[64,512,128]{2,1,0:T(8,128)(2,1)} %refs_2_.3, bf16[640,256]{1,0:T(8,128)(2,1)} %copy-done.1, bf16[640,256]{1,0:T(8,128)(2,1)} %copy-done.2), custom_call_target="tpu_custom_call" | custom-call | flops 1358954496 | bytes 4194304 | tf_op jit(solution)/shard_map/attend_0/pallas_call | solution.py:214
  67.8 1.5 collective-permute-start.9
  69.4 1.3 collective-permute-start.3
  70.7 1.0 collective-permute-start.2
  71.7 6.9 %attend_1.1.refs_0_ = bf16[32,4096]{1,0:T(8,128)(2,1)} custom-call(bf16[64,32,640]{2,1,0:T(8,128)(2,1)} %absorb.1.refs_0_, bf16[64,640]{1,0:T(8,128)(2,1)} %tree_keys.1.refs_1_, bf16[64,512,128]{2,1,0:T(8,128)(2,1)} %refs_2_.3, bf16[640,256]{1,0:T(8,128)(2,1)} %copy-done.1, bf16[640,256]{1,0:T(8,128)(2,1)} %copy-done.2), custom_call_target="tpu_custom_call" | custom-call | flops 1358954496 | bytes 4194304 | tf_op jit(solution)/shard_map/attend_1/pallas_call | solution.py:214
  78.6 0.8 collective-permute-start.24
  79.5 1.2 collective-permute-start.20
  80.7 1.4 collective-permute-done.5.refs_4_
  82.6 1.2 collective-permute-start.17
  83.8 2.0 %collective-permute-done.2.refs_1_ = bf16[32,4096]{1,0:T(8,128)(2,1)S(1)} collective-permute-done((bf16[32,4096]{1,0:T(8,128)(2,1)}, bf16[32,4096]{1,0:T(8,128)(2,1)S(1)}, u32[]{:S(2)}, u32[]{:S(2)}) %collective-permute-start.2) | collective-permute-done | bytes 262176 | tf_op jit(solution)/shard_map/ppermute | solution.py:22
  86.4 1.4 collective-permute-start.11
  87.8 5.2 %collective-permute-done.20.refs_4_ = bf16[32,4096]{1,0:T(8,128)(2,1)S(1)} collective-permute-done((bf16[32,4096]{1,0:T(8,128)(2,1)}, bf16[32,4096]{1,0:T(8,128)(2,1)S(1)}, u32[]{:S(2)}, u32[]{:S(2)}) %collective-permute-start.20) | collective-permute-done | bytes 262176 | tf_op jit(solution)/shard_map/ppermute | solution.py:22
  93.1 3.6 %collective-permute-done.17.refs_1_ = bf16[32,4096]{1,0:T(8,128)(2,1)S(1)} collective-permute-done((bf16[32,4096]{1,0:T(8,128)(2,1)}, bf16[32,4096]{1,0:T(8,128)(2,1)S(1)}, u32[]{:S(2)}, u32[]{:S(2)}) %collective-permute-start.17) | collective-permute-done | bytes 262176 | tf_op jit(solution)/shard_map/ppermute | solution.py:22
  97.7 5.0 %collective-permute-done.11.refs_2_ = bf16[32,4096]{1,0:T(8,128)(2,1)S(1)} collective-permute-done((bf16[32,4096]{1,0:T(8,128)(2,1)S(1)}, bf16[32,4096]{1,0:T(8,128)(2,1)S(1)}, u32[]{:S(2)}, u32[]{:S(2)}) %collective-permute-start.11) | collective-permute-done | bytes 262176 | tf_op jit(solution)/shard_map/ppermute | solution.py:22
  102.8 2.0 %collective-permute-start.26 = (bf16[32,4096]{1,0:T(8,128)(2,1)S(1)}, bf16[32,4096]{1,0:T(8,128)(2,1)S(1)}, u32[]{:S(2)}, u32[]{:S(2)}) collective-permute-start(bf16[32,4096]{1,0:T(8,128)(2,1)S(1)} %collective-permute-done.18.refs_2_), channel_id=1, source_target_pairs={{0,1},{1,0},{2,3},{3,2},{4,5},{5,4},{6,7},{7,6},{8,9},{9,8},{10,11... | collective-permute-start | bytes 786440 | tf_op jit(solution)/shard_map/ppermute | solution.py:22
  104.8 1.6 collective-permute-done.10.refs_1_
  106.3 1.3 collective-permute-done.6.refs_5_
  108.9 3.0 %collective-permute-done.28.refs_4_ = bf16[32,4096]{1,0:T(8,128)(2,1)S(1)} collective-permute-done((bf16[32,4096]{1,0:T(8,128)(2,1)S(1)}, bf16[32,4096]{1,0:T(8,128)(2,1)S(1)}, u32[]{:S(2)}, u32[]{:S(2)}) %collective-permute-start.28) | collective-permute-done | bytes 262176 | tf_op jit(solution)/shard_map/ppermute | solution.py:22
  111.9 1.4 collective-permute-start.8
  113.3 1.4 collective-permute-done.26.refs_2_
  114.7 0.9 collective-permute-start.15
  115.6 1.2 collective-permute-start.14
  116.8 4.4 %collective-permute-done.21.refs_5_ = bf16[32,4096]{1,0:T(8,128)(2,1)S(1)} collective-permute-done((bf16[32,4096]{1,0:T(8,128)(2,1)S(1)}, bf16[32,4096]{1,0:T(8,128)(2,1)S(1)}, u32[]{:S(2)}, u32[]{:S(2)}) %collective-permute-start.21) | collective-permute-done | bytes 262176 | tf_op jit(solution)/shard_map/ppermute | solution.py:22
  121.7 5.2 %collective-permute-done.8.refs_7_ = bf16[32,4096]{1,0:T(8,128)(2,1)} collective-permute-done((bf16[32,4096]{1,0:T(8,128)(2,1)}, bf16[32,4096]{1,0:T(8,128)(2,1)}, u32[]{:S(2)}, u32[]{:S(2)}) %collective-permute-start.8) | collective-permute-done | bytes 262176 | tf_op jit(solution)/shard_map/ppermute | solution.py:22
  128.1 1.8 %collective-permute-done.14.refs_5_ = bf16[32,4096]{1,0:T(8,128)(2,1)} collective-permute-done((bf16[32,4096]{1,0:T(8,128)(2,1)}, bf16[32,4096]{1,0:T(8,128)(2,1)}, u32[]{:S(2)}, u32[]{:S(2)}) %collective-permute-start.14) | collective-permute-done | bytes 262176 | tf_op jit(solution)/shard_map/ppermute | solution.py:22
  129.9 1.5 collective-permute-start.27
  131.3 3.6 %collective-permute-done.12.refs_3_ = bf16[32,4096]{1,0:T(8,128)(2,1)} collective-permute-done((bf16[32,4096]{1,0:T(8,128)(2,1)}, bf16[32,4096]{1,0:T(8,128)(2,1)}, u32[]{:S(2)}, u32[]{:S(2)}) %collective-permute-start.12) | collective-permute-done | bytes 262176 | tf_op jit(solution)/shard_map/ppermute | solution.py:22
  134.9 2.0 %collective-permute-start.30 = (bf16[32,4096]{1,0:T(8,128)(2,1)}, bf16[32,4096]{1,0:T(8,128)(2,1)}, u32[]{:S(2)}, u32[]{:S(2)}) collective-permute-start(bf16[32,4096]{1,0:T(8,128)(2,1)} %copy-done.16), channel_id=1, source_target_pairs={{0,1},{1,0},{2,3},{3,2},{4,5},{5,4},{6,7},{7,6},{8,9},{9,8},{10,11... | collective-permute-start | bytes 786440 | tf_op jit(solution)/shard_map/ppermute | solution.py:22
  137.8 2.1 %collective-permute-start.31 = (bf16[32,4096]{1,0:T(8,128)(2,1)}, bf16[32,4096]{1,0:T(8,128)(2,1)}, u32[]{:S(2)}, u32[]{:S(2)}) collective-permute-start(bf16[32,4096]{1,0:T(8,128)(2,1)} %collective-permute-done.23.refs_7_), channel_id=1, source_target_pairs={{0,1},{1,0},{2,3},{3,2},{4,5},{5,4},{6,7},{7,6},{8,9},{9,8},{10,11... | collective-permute-start | bytes 786440 | tf_op jit(solution)/shard_map/ppermute | solution.py:22
  139.8 5.3 %project_0.2.refs_1_ = f32[256,448]{1,0:T(8,128)} custom-call(bf16[32,4096]{1,0:T(8,128)(2,1)} %attend_0.1.refs_0_, bf16[32,4096]{1,0:T(8,128)(2,1)} %copy-done.7, bf16[32,4096]{1,0:T(8,128)(2,1)} %copy-done.6, bf16[32,4096]{1,0:T(8,128)(2,1)} %collective-permute-done.4.refs_3_, bf16[32,4096]{1,0:T(8,128)(2,1)} %copy-done.5, ...), custom_call_target="tpu_custom_call" | custom-call | flops 939524096 | bytes 3670016 | tf_op jit(solution)/shard_map/project_0/pallas_call | solution.py:247
  145.2 5.3 %project_1.2.refs_3_ = f32[256,448]{1,0:T(8,128)} custom-call(bf16[32,4096]{1,0:T(8,128)(2,1)} %attend_1.1.refs_0_, bf16[32,4096]{1,0:T(8,128)(2,1)} %copy-done.9, bf16[32,4096]{1,0:T(8,128)(2,1)} %copy-done.10, bf16[32,4096]{1,0:T(8,128)(2,1)} %collective-permute-done.19.refs_3_, bf16[32,4096]{1,0:T(8,128)(2,1)} %copy-done.8, bf16[32,4096]{1,0:T(8,128)(2,1)} %copy-done.17, ...), custom_call_target="tpu_custom_call" | custom-call | flops 939524096 | bytes 3670016 | tf_op jit(solution)/shard_map/project_1/pallas_call | solution.py:247
  150.5 5.3 %project_0.3.refs_2_ = f32[256,448]{1,0:T(8,128)} custom-call(bf16[32,4096]{1,0:T(8,128)(2,1)} %copy-done.4, bf16[32,4096]{1,0:T(8,128)(2,1)} %copy-done.14, bf16[32,4096]{1,0:T(8,128)(2,1)} %copy-done.12, bf16[32,4096]{1,0:T(8,128)(2,1)} %collective-permute-done.12.refs_3_, bf16[32,4096]{1,0:T(8,128)(2,1)} %copy-done.11, ...), custom_call_target="tpu_custom_call" | custom-call | flops 939524096 | bytes 3670016 | tf_op jit(solution)/shard_map/project_0/pallas_call | solution.py:247
  155.8 5.3 %project_1.3.refs_4_ = f32[256,448]{1,0:T(8,128)} custom-call(bf16[32,4096]{1,0:T(8,128)(2,1)} %copy-done.3, bf16[32,4096]{1,0:T(8,128)(2,1)} %collective-permute-done.25.refs_1_, bf16[32,4096]{1,0:T(8,128)(2,1)} %copy-done.15, bf16[32,4096]{1,0:T(8,128)(2,1)} %collective-permute-done.27.refs_3_, bf16[32,4096]{1,0:T(8,128)(2,1)} %copy-done.13, ...), custom_call_target="tpu_custom_call" | custom-call | flops 939524096 | bytes 3670016 | tf_op jit(solution)/shard_map/project_1/pallas_call | solution.py:247
  161.1 2.6 %collect.1 = f32[8,64,448]{2,1,0:T(8,128)} custom-call(s32[2]{0:T(128)} %pad_add_fusion.refs_0_, f32[256,448]{1,0:T(8,128)} %project_0.2.refs_1_, f32[256,448]{1,0:T(8,128)} %project_0.3.refs_2_, f32[256,448]{1,0:T(8,128)} %project_1.2.refs_3_, f32[256,448]{1,0:T(8,128)} %project_1.3.refs_4_), custom_call_target="tpu_custom_call" | custom-call | tf_op jit(solution)/shard_map/collect/pallas_call | solution.py:284
  163.7 1.1 dynamic-slice_convert_fusion
  164.9 1.5 collective-permute-done.32
  166.4 1.8 %add_convert_fusion = bf16[8,32,448]{2,1,0:T(8,128)(2,1)} fusion(bf16[8,32,448]{2,1,0:T(8,128)(2,1)S(1)} %collective-permute-done.32, f32[8,64,448]{2,1,0:T(8,128)} %collect.1, s32[]{:T(128)S(6)} %select_n.60), kind=kLoop, calls=%fused_computation.2 | loop fusion | flops 344064 | bytes 917508 | tf_op jit(solution)/shard_map/convert_element_type | solution.py:297
  (88 shorter events, 7.9 us)
Async XLA Ops:
  0.0 45.4 %copy-start = (bf16[1,64,64,128]{3,2,1,0:T(8,128)(2,1)S(1)}, bf16[1,64,64,128]{3,2,1,0:T(8,128)(2,1)}, u32[]{:S(2)}) copy-start(bf16[1,64,64,128]{3,2,1,0:T(8,128)(2,1)} %param.14) | copy-start | bytes 3145732
  2.6 23.9 %all-to-all-start = ((bf16[8,80,128]{2,1,0:T(8,128)(2,1)}), bf16[8,80,128]{2,1,0:T(8,128)(2,1)S(1)}, u32[]{:S(2)}, u32[]{:S(2)}) async-start(bf16[8,80,128]{2,1,0:T(8,128)(2,1)} %bitcast.11), calls=%async_computation | async-start | bytes 327680 | tf_op jit(solution)/shard_map/all_to_all | solution.py:164
  40.0 5.3 %collective-permute-start = (bf16[640,128]{1,0:T(8,128)(2,1)S(1)}, bf16[640,128]{1,0:T(8,128)(2,1)S(1)}, u32[]{:S(2)}, u32[]{:S(2)}) collective-permute-start(bf16[640,128]{1,0:T(8,128)(2,1)S(1)} %bitcast.36), channel_id=1, source_target_pairs={{0,16},{16,0},{1,17},{17,1},{2,18},{18,2},{3,19},{19,3},{4,20},{20... | collective-permute-start | bytes 491528 | tf_op jit(solution)/shard_map/ppermute | solution.py:22
  45.3 14.8 %copy-start.1 = (bf16[640,256]{1,0:T(8,128)(2,1)}, bf16[640,256]{1,0:T(8,128)(2,1)S(1)}, u32[]{:S(2)}) copy-start(bf16[640,256]{1,0:T(8,128)(2,1)S(1)} %pad_maximum_fusion.refs_3_) | copy-start | bytes 983044
  45.3 14.8 %collective-permute-start.1 = (bf16[640,256]{1,0:T(8,128)(2,1)S(1)}, bf16[640,256]{1,0:T(8,128)(2,1)S(1)}, u32[]{:S(2)}, u32[]{:S(2)}) collective-permute-start(bf16[640,256]{1,0:T(8,128)(2,1)S(1)} %pad_maximum_fusion.refs_3_), channel_id=1, source_target_pairs={{0,8},{8,0},{1,9},{9,1},{2,10},{10,2},{3,11},{11,3},{4,12},{12,4},... | collective-permute-start | bytes 983048 | tf_op jit(solution)/shard_map/ppermute | solution.py:22
  67.8 11.6 %collective-permute-start.9 = (bf16[32,4096]{1,0:T(8,128)(2,1)}, bf16[32,4096]{1,0:T(8,128)(2,1)S(1)}, u32[]{:S(2)}, u32[]{:S(2)}) collective-permute-start(bf16[32,4096]{1,0:T(8,128)(2,1)} %attend_0.1.refs_0_), channel_id=1, source_target_pairs={{0,16},{16,0},{1,17},{17,1},{2,18},{18,2},{3,19},{19,3},{4,20},{20... | collective-permute-start | bytes 786440 | tf_op jit(solution)/shard_map/ppermute | solution.py:22
  69.3 12.8 %collective-permute-start.5 = (bf16[32,4096]{1,0:T(8,128)(2,1)}, bf16[32,4096]{1,0:T(8,128)(2,1)S(1)}, u32[]{:S(2)}, u32[]{:S(2)}) collective-permute-start(bf16[32,4096]{1,0:T(8,128)(2,1)} %attend_0.1.refs_0_), channel_id=1, source_target_pairs={{0,2},{1,3},{2,0},{3,1},{4,6},{5,7},{6,4},{7,5},{8,10},{9,11},{10,... | collective-permute-start | bytes 786440 | tf_op jit(solution)/shard_map/ppermute | solution.py:22
  69.4 13.3 %collective-permute-start.3 = (bf16[32,4096]{1,0:T(8,128)(2,1)}, bf16[32,4096]{1,0:T(8,128)(2,1)S(1)}, u32[]{:S(2)}, u32[]{:S(2)}) collective-permute-start(bf16[32,4096]{1,0:T(8,128)(2,1)} %attend_0.1.refs_0_), channel_id=1, source_target_pairs={{0,1},{1,0},{2,3},{3,2},{4,5},{5,4},{6,7},{7,6},{8,9},{9,8},{10,11... | collective-permute-start | bytes 786440 | tf_op jit(solution)/shard_map/ppermute | solution.py:22
  70.7 15.1 %collective-permute-start.2 = (bf16[32,4096]{1,0:T(8,128)(2,1)}, bf16[32,4096]{1,0:T(8,128)(2,1)S(1)}, u32[]{:S(2)}, u32[]{:S(2)}) collective-permute-start(bf16[32,4096]{1,0:T(8,128)(2,1)} %attend_0.1.refs_0_), channel_id=1, source_target_pairs={{0,4},{1,5},{2,6},{3,7},{4,0},{5,1},{6,2},{7,3},{8,12},{9,13},{10,... | collective-permute-start | bytes 786440 | tf_op jit(solution)/shard_map/ppermute | solution.py:22
  78.6 7.8 %collective-permute-start.24 = (bf16[32,4096]{1,0:T(8,128)(2,1)}, bf16[32,4096]{1,0:T(8,128)(2,1)S(1)}, u32[]{:S(2)}, u32[]{:S(2)}) collective-permute-start(bf16[32,4096]{1,0:T(8,128)(2,1)} %attend_1.1.refs_0_), channel_id=1, source_target_pairs={{0,1},{1,0},{2,3},{3,2},{4,5},{5,4},{6,7},{7,6},{8,9},{9,8},{10,11... | collective-permute-start | bytes 786440 | tf_op jit(solution)/shard_map/ppermute | solution.py:22
  79.4 71.0 %copy-start.4 = (bf16[32,4096]{1,0:T(8,128)(2,1)}, bf16[32,4096]{1,0:T(8,128)(2,1)S(1)}, u32[]{:S(2)}) copy-start(bf16[32,4096]{1,0:T(8,128)(2,1)S(1)} %collective-permute-done.9.refs_0_) | copy-start | bytes 786436
  79.5 13.5 %collective-permute-start.20 = (bf16[32,4096]{1,0:T(8,128)(2,1)}, bf16[32,4096]{1,0:T(8,128)(2,1)S(1)}, u32[]{:S(2)}, u32[]{:S(2)}) collective-permute-start(bf16[32,4096]{1,0:T(8,128)(2,1)} %attend_1.1.refs_0_), channel_id=1, source_target_pairs={{0,2},{1,3},{2,0},{3,1},{4,6},{5,7},{6,4},{7,5},{8,10},{9,11},{10,... | collective-permute-start | bytes 786440 | tf_op jit(solution)/shard_map/ppermute | solution.py:22
  82.1 57.7 %copy-start.5 = (bf16[32,4096]{1,0:T(8,128)(2,1)}, bf16[32,4096]{1,0:T(8,128)(2,1)S(1)}, u32[]{:S(2)}) copy-start(bf16[32,4096]{1,0:T(8,128)(2,1)S(1)} %collective-permute-done.5.refs_4_) | copy-start | bytes 786436
  82.1 10.8 %collective-permute-start.18 = (bf16[32,4096]{1,0:T(8,128)(2,1)}, bf16[32,4096]{1,0:T(8,128)(2,1)S(1)}, u32[]{:S(2)}, u32[]{:S(2)}) collective-permute-start(bf16[32,4096]{1,0:T(8,128)(2,1)} %attend_1.1.refs_0_), channel_id=1, source_target_pairs={{0,16},{16,0},{1,17},{17,1},{2,18},{18,2},{3,19},{19,3},{4,20},{20... | collective-permute-start | bytes 786440 | tf_op jit(solution)/shard_map/ppermute | solution.py:22
  82.6 57.2 %copy-start.6 = (bf16[32,4096]{1,0:T(8,128)(2,1)}, bf16[32,4096]{1,0:T(8,128)(2,1)S(1)}, u32[]{:S(2)}) copy-start(bf16[32,4096]{1,0:T(8,128)(2,1)S(1)} %collective-permute-done.3.refs_2_) | copy-start | bytes 786436
  82.6 14.0 %collective-permute-start.17 = (bf16[32,4096]{1,0:T(8,128)(2,1)}, bf16[32,4096]{1,0:T(8,128)(2,1)S(1)}, u32[]{:S(2)}, u32[]{:S(2)}) collective-permute-start(bf16[32,4096]{1,0:T(8,128)(2,1)} %attend_1.1.refs_0_), channel_id=1, source_target_pairs={{0,4},{1,5},{2,6},{3,7},{4,0},{5,1},{6,2},{7,3},{8,12},{9,13},{10,... | collective-permute-start | bytes 786440 | tf_op jit(solution)/shard_map/ppermute | solution.py:22
  85.8 54.1 %copy-start.7 = (bf16[32,4096]{1,0:T(8,128)(2,1)}, bf16[32,4096]{1,0:T(8,128)(2,1)S(1)}, u32[]{:S(2)}) copy-start(bf16[32,4096]{1,0:T(8,128)(2,1)S(1)} %collective-permute-done.2.refs_1_) | copy-start | bytes 786436
  85.8 11.4 %collective-permute-start.13 = (bf16[32,4096]{1,0:T(8,128)(2,1)S(1)}, bf16[32,4096]{1,0:T(8,128)(2,1)S(1)}, u32[]{:S(2)}, u32[]{:S(2)}) collective-permute-start(bf16[32,4096]{1,0:T(8,128)(2,1)S(1)} %collective-permute-done.5.refs_4_), channel_id=1, source_target_pairs={{0,16},{16,0},{1,17},{17,1},{2,18},{18,2},{3,19},{19,3},{4,20},{20... | collective-permute-start | bytes 786440 | tf_op jit(solution)/shard_map/ppermute | solution.py:22
  86.4 64.0 %copy-start.3 = (bf16[32,4096]{1,0:T(8,128)(2,1)}, bf16[32,4096]{1,0:T(8,128)(2,1)S(1)}, u32[]{:S(2)}) copy-start(bf16[32,4096]{1,0:T(8,128)(2,1)S(1)} %collective-permute-done.24.refs_0_) | copy-start | bytes 786436
  86.4 16.3 %collective-permute-start.11 = (bf16[32,4096]{1,0:T(8,128)(2,1)S(1)}, bf16[32,4096]{1,0:T(8,128)(2,1)S(1)}, u32[]{:S(2)}, u32[]{:S(2)}) collective-permute-start(bf16[32,4096]{1,0:T(8,128)(2,1)S(1)} %collective-permute-done.3.refs_2_), channel_id=1, source_target_pairs={{0,16},{16,0},{1,17},{17,1},{2,18},{18,2},{3,19},{19,3},{4,20},{20... | collective-permute-start | bytes 786440 | tf_op jit(solution)/shard_map/ppermute | solution.py:22
  93.0 52.2 %copy-start.8 = (bf16[32,4096]{1,0:T(8,128)(2,1)}, bf16[32,4096]{1,0:T(8,128)(2,1)S(1)}, u32[]{:S(2)}) copy-start(bf16[32,4096]{1,0:T(8,128)(2,1)S(1)} %collective-permute-done.20.refs_4_) | copy-start | bytes 786436
  93.0 9.8 %collective-permute-start.7 = (bf16[32,4096]{1,0:T(8,128)(2,1)S(1)}, bf16[32,4096]{1,0:T(8,128)(2,1)}, u32[]{:S(2)}, u32[]{:S(2)}) collective-permute-start(bf16[32,4096]{1,0:T(8,128)(2,1)S(1)} %collective-permute-done.3.refs_2_), channel_id=1, source_target_pairs={{0,2},{1,3},{2,0},{3,1},{4,6},{5,7},{6,4},{7,5},{8,10},{9,11},{10,... | collective-permute-start | bytes 786440 | tf_op jit(solution)/shard_map/ppermute | solution.py:22
  93.0 52.2 %copy-start.10 = (bf16[32,4096]{1,0:T(8,128)(2,1)}, bf16[32,4096]{1,0:T(8,128)(2,1)S(1)}, u32[]{:S(2)}) copy-start(bf16[32,4096]{1,0:T(8,128)(2,1)S(1)} %collective-permute-done.18.refs_2_) | copy-start | bytes 786436
  93.0 13.4 %collective-permute-start.10 = (bf16[32,4096]{1,0:T(8,128)(2,1)S(1)}, bf16[32,4096]{1,0:T(8,128)(2,1)S(1)}, u32[]{:S(2)}, u32[]{:S(2)}) collective-permute-start(bf16[32,4096]{1,0:T(8,128)(2,1)S(1)} %collective-permute-done.2.refs_1_), channel_id=1, source_target_pairs={{0,16},{16,0},{1,17},{17,1},{2,18},{18,2},{3,19},{19,3},{4,20},{20... | collective-permute-start | bytes 786440 | tf_op jit(solution)/shard_map/ppermute | solution.py:22
  96.7 48.5 %copy-start.9 = (bf16[32,4096]{1,0:T(8,128)(2,1)}, bf16[32,4096]{1,0:T(8,128)(2,1)S(1)}, u32[]{:S(2)}) copy-start(bf16[32,4096]{1,0:T(8,128)(2,1)S(1)} %collective-permute-done.17.refs_1_) | copy-start | bytes 786436
  96.7 10.9 %collective-permute-start.6 = (bf16[32,4096]{1,0:T(8,128)(2,1)S(1)}, bf16[32,4096]{1,0:T(8,128)(2,1)}, u32[]{:S(2)}, u32[]{:S(2)}) collective-permute-start(bf16[32,4096]{1,0:T(8,128)(2,1)S(1)} %collective-permute-done.2.refs_1_), channel_id=1, source_target_pairs={{0,2},{1,3},{2,0},{3,1},{4,6},{5,7},{6,4},{7,5},{8,10},{9,11},{10,... | collective-permute-start | bytes 786440 | tf_op jit(solution)/shard_map/ppermute | solution.py:22
  97.1 53.3 %copy-start.11 = (bf16[32,4096]{1,0:T(8,128)(2,1)}, bf16[32,4096]{1,0:T(8,128)(2,1)S(1)}, u32[]{:S(2)}) copy-start(bf16[32,4096]{1,0:T(8,128)(2,1)S(1)} %collective-permute-done.13.refs_4_) | copy-start | bytes 786436
  97.1 11.2 %collective-permute-start.4 = (bf16[32,4096]{1,0:T(8,128)(2,1)S(1)}, bf16[32,4096]{1,0:T(8,128)(2,1)}, u32[]{:S(2)}, u32[]{:S(2)}) collective-permute-start(bf16[32,4096]{1,0:T(8,128)(2,1)S(1)} %collective-permute-done.2.refs_1_), channel_id=1, source_target_pairs={{0,1},{1,0},{2,3},{3,2},{4,5},{5,4},{6,7},{7,6},{8,9},{9,8},{10,11... | collective-permute-start | bytes 786440 | tf_op jit(solution)/shard_map/ppermute | solution.py:22
  102.8 18.9 %copy-start.12 = (bf16[32,4096]{1,0:T(8,128)(2,1)}, bf16[32,4096]{1,0:T(8,128)(2,1)S(1)}, u32[]{:S(2)}) copy-start(bf16[32,4096]{1,0:T(8,128)(2,1)S(1)} %collective-permute-done.11.refs_2_) | copy-start | bytes 786436
  102.8 9.2 %collective-permute-start.28 = (bf16[32,4096]{1,0:T(8,128)(2,1)S(1)}, bf16[32,4096]{1,0:T(8,128)(2,1)S(1)}, u32[]{:S(2)}, u32[]{:S(2)}) collective-permute-start(bf16[32,4096]{1,0:T(8,128)(2,1)S(1)} %collective-permute-done.20.refs_4_), channel_id=1, source_target_pairs={{0,1},{1,0},{2,3},{3,2},{4,5},{5,4},{6,7},{7,6},{8,9},{9,8},{10,11... | collective-permute-start | bytes 786440 | tf_op jit(solution)/shard_map/ppermute | solution.py:22
  102.8 12.0 %collective-permute-start.26 = (bf16[32,4096]{1,0:T(8,128)(2,1)S(1)}, bf16[32,4096]{1,0:T(8,128)(2,1)S(1)}, u32[]{:S(2)}, u32[]{:S(2)}) collective-permute-start(bf16[32,4096]{1,0:T(8,128)(2,1)S(1)} %collective-permute-done.18.refs_2_), channel_id=1, source_target_pairs={{0,1},{1,0},{2,3},{3,2},{4,5},{5,4},{6,7},{7,6},{8,9},{9,8},{10,11... | collective-permute-start | bytes 786440 | tf_op jit(solution)/shard_map/ppermute | solution.py:22
  106.3 20.5 %copy-start.14 = (bf16[32,4096]{1,0:T(8,128)(2,1)}, bf16[32,4096]{1,0:T(8,128)(2,1)S(1)}, u32[]{:S(2)}) copy-start(bf16[32,4096]{1,0:T(8,128)(2,1)S(1)} %collective-permute-done.10.refs_1_) | copy-start | bytes 786436
  106.3 9.3 %collective-permute-start.22 = (bf16[32,4096]{1,0:T(8,128)(2,1)S(1)}, bf16[32,4096]{1,0:T(8,128)(2,1)S(1)}, u32[]{:S(2)}, u32[]{:S(2)}) collective-permute-start(bf16[32,4096]{1,0:T(8,128)(2,1)S(1)} %collective-permute-done.18.refs_2_), channel_id=1, source_target_pairs={{0,2},{1,3},{2,0},{3,1},{4,6},{5,7},{6,4},{7,5},{8,10},{9,11},{10,... | collective-permute-start | bytes 786440 | tf_op jit(solution)/shard_map/ppermute | solution.py:22
  107.6 13.5 %collective-permute-start.21 = (bf16[32,4096]{1,0:T(8,128)(2,1)S(1)}, bf16[32,4096]{1,0:T(8,128)(2,1)S(1)}, u32[]{:S(2)}, u32[]{:S(2)}) collective-permute-start(bf16[32,4096]{1,0:T(8,128)(2,1)S(1)} %collective-permute-done.17.refs_1_), channel_id=1, source_target_pairs={{0,2},{1,3},{2,0},{3,1},{4,6},{5,7},{6,4},{7,5},{8,10},{9,11},{10,... | collective-permute-start | bytes 786440 | tf_op jit(solution)/shard_map/ppermute | solution.py:22
  108.4 13.3 %collective-permute-start.19 = (bf16[32,4096]{1,0:T(8,128)(2,1)S(1)}, bf16[32,4096]{1,0:T(8,128)(2,1)}, u32[]{:S(2)}, u32[]{:S(2)}) collective-permute-start(bf16[32,4096]{1,0:T(8,128)(2,1)S(1)} %collective-permute-done.17.refs_1_), channel_id=1, source_target_pairs={{0,16},{16,0},{1,17},{17,1},{2,18},{18,2},{3,19},{19,3},{4,20},{20... | collective-permute-start | bytes 786440 | tf_op jit(solution)/shard_map/ppermute | solution.py:22
  111.9 14.9 %collective-permute-start.8 = (bf16[32,4096]{1,0:T(8,128)(2,1)}, bf16[32,4096]{1,0:T(8,128)(2,1)}, u32[]{:S(2)}, u32[]{:S(2)}) collective-permute-start(bf16[32,4096]{1,0:T(8,128)(2,1)} %collective-permute-done.4.refs_3_), channel_id=1, source_target_pairs={{0,2},{1,3},{2,0},{3,1},{4,6},{5,7},{6,4},{7,5},{8,10},{9,11},{10,... | collective-permute-start | bytes 786440 | tf_op jit(solution)/shard_map/ppermute | solution.py:22
  114.7 12.1 %copy-start.15 = (bf16[32,4096]{1,0:T(8,128)(2,1)}, bf16[32,4096]{1,0:T(8,128)(2,1)S(1)}, u32[]{:S(2)}) copy-start(bf16[32,4096]{1,0:T(8,128)(2,1)S(1)} %collective-permute-done.26.refs_2_) | copy-start | bytes 786436
  114.7 13.3 %collective-permute-start.15 = (bf16[32,4096]{1,0:T(8,128)(2,1)}, bf16[32,4096]{1,0:T(8,128)(2,1)}, u32[]{:S(2)}, u32[]{:S(2)}) collective-permute-start(bf16[32,4096]{1,0:T(8,128)(2,1)} %collective-permute-done.7.refs_6_), channel_id=1, source_target_pairs={{0,16},{16,0},{1,17},{17,1},{2,18},{18,2},{3,19},{19,3},{4,20},{20... | collective-permute-start | bytes 786440 | tf_op jit(solution)/shard_map/ppermute | solution.py:22
  115.6 14.2 %collective-permute-start.14 = (bf16[32,4096]{1,0:T(8,128)(2,1)}, bf16[32,4096]{1,0:T(8,128)(2,1)}, u32[]{:S(2)}, u32[]{:S(2)}) collective-permute-start(bf16[32,4096]{1,0:T(8,128)(2,1)} %collective-permute-done.6.refs_5_), channel_id=1, source_target_pairs={{0,16},{16,0},{1,17},{17,1},{2,18},{18,2},{3,19},{19,3},{4,20},{20... | collective-permute-start | bytes 786440 | tf_op jit(solution)/shard_map/ppermute | solution.py:22
  121.1 13.8 %collective-permute-start.12 = (bf16[32,4096]{1,0:T(8,128)(2,1)}, bf16[32,4096]{1,0:T(8,128)(2,1)}, u32[]{:S(2)}, u32[]{:S(2)}) collective-permute-start(bf16[32,4096]{1,0:T(8,128)(2,1)} %collective-permute-done.4.refs_3_), channel_id=1, source_target_pairs={{0,16},{16,0},{1,17},{17,1},{2,18},{18,2},{3,19},{19,3},{4,20},{20... | collective-permute-start | bytes 786440 | tf_op jit(solution)/shard_map/ppermute | solution.py:22
  121.7 15.3 %collective-permute-start.23 = (bf16[32,4096]{1,0:T(8,128)(2,1)}, bf16[32,4096]{1,0:T(8,128)(2,1)}, u32[]{:S(2)}, u32[]{:S(2)}) collective-permute-start(bf16[32,4096]{1,0:T(8,128)(2,1)} %collective-permute-done.19.refs_3_), channel_id=1, source_target_pairs={{0,2},{1,3},{2,0},{3,1},{4,6},{5,7},{6,4},{7,5},{8,10},{9,11},{10,... | collective-permute-start | bytes 786440 | tf_op jit(solution)/shard_map/ppermute | solution.py:22
  126.9 10.9 %collective-permute-start.16 = (bf16[32,4096]{1,0:T(8,128)(2,1)}, bf16[32,4096]{1,0:T(8,128)(2,1)}, u32[]{:S(2)}, u32[]{:S(2)}) collective-permute-start(bf16[32,4096]{1,0:T(8,128)(2,1)} %collective-permute-done.8.refs_7_), channel_id=1, source_target_pairs={{0,16},{16,0},{1,17},{17,1},{2,18},{18,2},{3,19},{19,3},{4,20},{20... | collective-permute-start | bytes 786440 | tf_op jit(solution)/shard_map/ppermute | solution.py:22
  128.1 27.7 %collective-permute-start.25 = (bf16[32,4096]{1,0:T(8,128)(2,1)S(1)}, bf16[32,4096]{1,0:T(8,128)(2,1)}, u32[]{:S(2)}, u32[]{:S(2)}) collective-permute-start(bf16[32,4096]{1,0:T(8,128)(2,1)S(1)} %collective-permute-done.17.refs_1_), channel_id=1, source_target_pairs={{0,1},{1,0},{2,3},{3,2},{4,5},{5,4},{6,7},{7,6},{8,9},{9,8},{10,11... | collective-permute-start | bytes 786440 | tf_op jit(solution)/shard_map/ppermute | solution.py:22
  129.9 25.9 %collective-permute-start.27 = (bf16[32,4096]{1,0:T(8,128)(2,1)}, bf16[32,4096]{1,0:T(8,128)(2,1)}, u32[]{:S(2)}, u32[]{:S(2)}) collective-permute-start(bf16[32,4096]{1,0:T(8,128)(2,1)} %collective-permute-done.19.refs_3_), channel_id=1, source_target_pairs={{0,1},{1,0},{2,3},{3,2},{4,5},{5,4},{6,7},{7,6},{8,9},{9,8},{10,11... | collective-permute-start | bytes 786440 | tf_op jit(solution)/shard_map/ppermute | solution.py:22
  134.9 20.8 %collective-permute-start.30 = (bf16[32,4096]{1,0:T(8,128)(2,1)}, bf16[32,4096]{1,0:T(8,128)(2,1)}, u32[]{:S(2)}, u32[]{:S(2)}) collective-permute-start(bf16[32,4096]{1,0:T(8,128)(2,1)} %copy-done.16), channel_id=1, source_target_pairs={{0,1},{1,0},{2,3},{3,2},{4,5},{5,4},{6,7},{7,6},{8,9},{9,8},{10,11... | collective-permute-start | bytes 786440 | tf_op jit(solution)/shard_map/ppermute | solution.py:22
  136.9 18.8 %collective-permute-start.29 = (bf16[32,4096]{1,0:T(8,128)(2,1)}, bf16[32,4096]{1,0:T(8,128)(2,1)}, u32[]{:S(2)}, u32[]{:S(2)}) collective-permute-start(bf16[32,4096]{1,0:T(8,128)(2,1)} %copy-done.17), channel_id=1, source_target_pairs={{0,1},{1,0},{2,3},{3,2},{4,5},{5,4},{6,7},{7,6},{8,9},{9,8},{10,11... | collective-permute-start | bytes 786440 | tf_op jit(solution)/shard_map/ppermute | solution.py:22
  137.8 18.0 %collective-permute-start.31 = (bf16[32,4096]{1,0:T(8,128)(2,1)}, bf16[32,4096]{1,0:T(8,128)(2,1)}, u32[]{:S(2)}, u32[]{:S(2)}) collective-permute-start(bf16[32,4096]{1,0:T(8,128)(2,1)} %collective-permute-done.23.refs_7_), channel_id=1, source_target_pairs={{0,1},{1,0},{2,3},{3,2},{4,5},{5,4},{6,7},{7,6},{8,9},{9,8},{10,11... | collective-permute-start | bytes 786440 | tf_op jit(solution)/shard_map/ppermute | solution.py:22
  164.8 1.6 collective-permute-start.32
  (4 other events, 27.5 us)
